TPU v7x, 32 devices: a whole 2x2x4 slice. The times are simulated.
32 devices in a mesh: member: 4 (over z), lat: 4 (over y, core), lon: 2 (over x).
Axes of the slice: x: 2, y: 2, z: 4, core: 2. Of those that a mesh axis runs over, the one named last changes fastest.
Arguments:
- state: bfloat16 [100, 8, 720], P(None, 'lat', 'lon'), may hold values from -6 to 6
- target: bfloat16 [100, 8, 720], P(None, 'lat', 'lon'), may hold values from -6 to 6
- land_sea: int32 [8, 720], P('lat', 'lon'), may hold values 0 or 1
- seeds: int32 [4, 32], P('member'), may hold values from 0 to 65535
- w_in: bfloat16 [9, 100, 256], replicated, may hold values from -0.1875 to 0.1875
- w_mid: bfloat16 [9, 256, 256], replicated, may hold values from -0.125 to 0.125
- w_out: bfloat16 [100, 256], replicated, may hold values from -0.375 to 0.375
- w_noise: float32 [32, 256], replicated, may hold values from -1 to 1
Outputs:
- update_in: float32 [9, 100, 256], replicated
- update_mid: float32 [9, 256, 256], replicated
- update_out: float32 [100, 256], replicated
- update_noise: float32 [32, 256], replicated
- loss: float32 [], replicated
All inputs are finite; a program needn't handle non-finite values. No bound on the sum of `land_sea` on one device may be relied on, other than what follows from the above.
Results may differ from a plain program's by a relative error of at most 0.0014.
Values may be sent and summed in bfloat16 or wider, within the bound.
A program may use at most 64 MiB of HBM per device.

v0:
```python
import jax
import jax.numpy as jnp
from jax import lax
from jax.sharding import PartitionSpec as P

SMOOTH = 0.25


def with_halo(block, sides, width):
    for axis, dim in sides:
        count = lax.axis_size(axis)
        forward = [(i, i + 1) for i in range(count - 1)]
        forward.append((count - 1, 0))
        backward = [(target, source) for source, target in forward]
        low = lax.ppermute(
            lax.slice_in_dim(block, block.shape[dim] - width, None, axis=dim), axis, forward
        )
        high = lax.ppermute(lax.slice_in_dim(block, 0, width, axis=dim), axis, backward)
        block = jnp.concatenate([low, block, high], axis=dim)
    return block


def shifted(padded, offset, row_count, col_count):
    row_shift = offset // 3
    col_shift = offset % 3
    window = padded[:, row_shift : row_shift + row_count, col_shift : col_shift + col_count]
    return window.reshape(padded.shape[0], row_count * col_count)


def conv_forward(weights, padded, row_count, col_count):
    summed = None
    for offset in range(9):
        window = shifted(padded, offset, row_count, col_count)
        part = lax.dot_general(
            weights[offset], window, (((0,), (0,)), ((), ())), preferred_element_type=jnp.float32
        )
        summed = part if summed is None else summed + part
    return summed


def conv_back(weights, padded, row_count, col_count):
    summed = None
    for offset in range(9):
        window = shifted(padded, 8 - offset, row_count, col_count)
        part = jnp.dot(weights[offset], window, preferred_element_type=jnp.float32)
        summed = part if summed is None else summed + part
    return summed


def weight_grad(padded, deltas, row_count, col_count):
    parts = []
    for offset in range(9):
        window = shifted(padded, offset, row_count, col_count)
        parts.append(
            lax.dot_general(
                window, deltas, (((1,), (1,)), ((), ())), preferred_element_type=jnp.float32
            )
        )
    return jnp.stack(parts)


def gelu_pair(pre):
    return jax.jvp(jax.nn.gelu, (pre,), (jnp.ones_like(pre),))


def clear_outside(padded, width, lat_index, lat_count):
    row_count = padded.shape[1] - 2 * width
    global_row = lat_index * row_count + jnp.arange(padded.shape[1], dtype=jnp.int32) - width
    inside = (global_row >= 0) & (global_row < row_count * lat_count)
    return jnp.where(inside[None, :, None], padded, jnp.zeros((), padded.dtype))


def combine(outputs, target_flat, weights, slope_sum, spread_sum, members):
    misses = outputs - target_flat[None]
    radius = jnp.sqrt(misses * misses + SMOOTH * SMOOTH)
    gradients = weights[None] * (misses / radius / members - slope_sum / (members * (members - 1)))
    loss_term = jnp.sum(
        weights[None] * ((radius - SMOOTH) / members - spread_sum / (2 * members * (members - 1)))
    )
    return (gradients, loss_term)


def pair_sums(outputs, others, running):

    def add_member(totals, member_out):
        gap_value = outputs - member_out.astype(jnp.float32)[None]
        radius = jnp.sqrt(gap_value * gap_value + SMOOTH * SMOOTH)
        return ((totals[0] + gap_value / radius, totals[1] + radius - SMOOTH), None)

    sums, _ = lax.scan(add_member, running, others)
    return sums


def normalize(gradient):
    return gradient / jnp.sqrt(jnp.mean(gradient * gradient) + 1e-06)


def body(state, target, land_sea, seeds, w_in, w_mid, w_out, w_noise):
    variables, row_count, col_count = state.shape
    channels = w_in.shape[2]
    cell_count = row_count * col_count
    lat_index = lax.axis_index("lat")
    lat_count = lax.axis_size("lat")
    members = lax.axis_size("member")
    latent = (seeds[0].astype(jnp.float32) - 32767.5) / 18918.0
    noise_bias = jnp.dot(latent, w_noise, precision=lax.Precision.HIGHEST)
    state_pad = with_halo(state, (("lat", 1), ("lon", 2)), 1)
    state_pad = clear_outside(state_pad, 1, lat_index, lat_count)
    pre_in = conv_forward(w_in, state_pad, row_count, col_count) + noise_bias[:, None]
    act_in, slope_in = gelu_pair(pre_in)
    hidden_in = act_in.astype(jnp.bfloat16)
    hidden_pad = with_halo(
        hidden_in.reshape(channels, row_count, col_count), (("lat", 1), ("lon", 2)), 1
    )
    hidden_pad = clear_outside(hidden_pad, 1, lat_index, lat_count)
    pre_mid = conv_forward(w_mid, hidden_pad, row_count, col_count)
    act_mid, slope_mid = gelu_pair(pre_mid)
    hidden_out = (act_mid + hidden_in.astype(jnp.float32)).astype(jnp.bfloat16)
    flat_state = state.reshape(variables, cell_count).astype(jnp.float32)
    output = (flat_state + jnp.dot(w_out, hidden_out, preferred_element_type=jnp.float32)).astype(
        jnp.bfloat16
    )
    target_flat = target.reshape(variables, cell_count).astype(jnp.float32)
    weights = 1.0 + land_sea.reshape(1, cell_count).astype(jnp.float32)
    own_output = output.astype(jnp.float32)[None]
    blank = jnp.zeros(own_output.shape, jnp.float32)
    slope_sum, spread_sum = pair_sums(
        own_output, lax.all_gather(output[None], "member", axis=0, tiled=True), (blank, blank)
    )
    gradients, loss_term = combine(own_output, target_flat, weights, slope_sum, spread_sum, members)
    delta_out = gradients[0].astype(jnp.bfloat16)
    grad_out = lax.dot_general(
        delta_out, hidden_out, (((1,), (1,)), ((), ())), preferred_element_type=jnp.float32
    )
    upstream = lax.dot_general(
        w_out, delta_out, (((0,), (0,)), ((), ())), preferred_element_type=jnp.float32
    )
    delta_mid = (upstream * slope_mid).astype(jnp.bfloat16)
    delta_pad = with_halo(
        delta_mid.reshape(channels, row_count, col_count), (("lat", 1), ("lon", 2)), 1
    )
    delta_pad = clear_outside(delta_pad, 1, lat_index, lat_count)
    incoming = conv_back(w_mid, delta_pad, row_count, col_count) + upstream
    delta_in = (incoming * slope_in).astype(jnp.bfloat16)
    grad_mid = weight_grad(hidden_pad, delta_mid, row_count, col_count)
    grad_in = weight_grad(state_pad, delta_in, row_count, col_count)
    grad_noise = latent[:, None] * jnp.sum(delta_in.astype(jnp.float32), axis=1)[None, :]
    grad_in, grad_mid, grad_out, grad_noise, summed = lax.psum(
        (grad_in, grad_mid, grad_out, grad_noise, loss_term), ("member", "lat", "lon")
    )
    loss = summed / (variables * cell_count * lat_count * lax.axis_size("lon"))
    return (
        normalize(grad_in),
        normalize(grad_mid),
        normalize(grad_out),
        normalize(grad_noise),
        loss,
    )


def solution(mesh):
    placed = (
        P(None, "lat", "lon"),
        P(None, "lat", "lon"),
        P("lat", "lon"),
        P("member", None),
        P(),
        P(),
        P(),
        P(),
    )
    return jax.shard_map(
        body, mesh=mesh, in_specs=placed, out_specs=(P(), P(), P(), P(), P()), check_vma=False
    )
```

profile of v0, /device:TPU:0, one launch (start us, length us, event | category | flops | bytes accessed | tf_op | source)
XLA Modules:
  0.0 255.6 jit_solution(3920980561953618674)
XLA Ops:
  8.5 2.5 collective-permute-start.1
  11.9 3.4 %collective-permute-done.1 = bf16[100,1,360]{2,1,0:T(2,128)(2,1)S(1)} collective-permute-done((bf16[100,1,360]{2,1,0:T(2,128)(2,1)S(1)}, bf16[100,1,360]{2,1,0:T(2,128)(2,1)S(1)}, u32[]{:S(2)}, u32[]{:S(2)}) %collective-permute-start.1) | collective-permute-done | bytes 72032 | tf_op jit(solution)/shard_map/ppermute | solution.py:18
  16.4 1.3 pad_maximum_fusion.2
  17.7 1.6 collective-permute-start.3
  19.8 3.2 %collective-permute-done.3 = bf16[100,4,1]{2,1,0:T(4,128)(2,1)S(1)} collective-permute-done((bf16[100,4,1]{2,1,0:T(4,128)(2,1)S(1)}, bf16[100,4,1]{2,1,0:T(4,128)(2,1)S(1)}, u32[]{:S(2)}, u32[]{:S(2)}) %collective-permute-start.3) | collective-permute-done | bytes 832 | tf_op jit(solution)/shard_map/ppermute | solution.py:18
  24.1 2.2 maximum_select_fusion.2
  26.3 1.4 fusion.123
  31.7 1.3 multiply_convert_fusion
  34.1 4.3 %collective-permute-done.5 = bf16[256,1,360]{0,2,1:T(8,128)(2,1)S(1)} collective-permute-done((bf16[256,1,360]{0,2,1:T(8,128)(2,1)S(1)}, bf16[256,1,360]{0,2,1:T(8,128)(2,1)S(1)}, u32[]{:S(2)}, u32[]{:S(2)}) %collective-permute-start.5) | collective-permute-done | bytes 184352 | tf_op jit(solution)/shard_map/ppermute | solution.py:18
  38.4 2.3 collective-permute-done.4
  40.8 1.6 collective-permute-start.7
  44.7 1.3 collective-permute-done.6
  49.8 1.3 add_convert_fusion
  51.4 16.8 %all-gather.1 = bf16[4,100,720]{2,1,0:T(8,128)(2,1)} all-gather(bf16[1,100,720]{2,1,0:T(8,128)(2,1)S(1)} %bitcast.306), channel_id=2, replica_groups=mesh['member'=4,'lat'=4,'lon'=2] {'member'}, dimensions={0}, use_global_device_ids=true | all-gather | bytes 720000 | tf_op jit(solution)/shard_map/all_gather | solution.py:128
  68.2 4.7 %while.15 = (s32[]{:T(128)}, f32[1,100,720]{2,1,0:T(8,128)S(1)}, f32[1,100,720]{2,1,0:T(8,128)S(1)}, bf16[4,100,720]{2,1,0:T(8,128)(2,1)}, f32[1,100,720]{2,1,0:T(8,128)S(1)}, /*index=5*/s32[]{:T(128)}, s32[]{:T(128)}) while((s32[]{:T(128)}, f32[1,100,720]{2,1,0:T(8,128)S(1)}, f32[1,100,720]{2,1,0:T(8,128)S(1)}, ...), condition=%wide.region_1.2_spmd.clone, body=%wide.region_0.1_spmd.clone.sunk | while | flops 720003 | bytes 1584099 | solution.py:90
  72.9 1.8 fusion.51
  74.8 1.7 fusion.49
  81.2 2.4 collective-permute-done.8
  83.8 2.0 collective-permute-start.10
  95.2 40.8 %all-reduce = (f32[32,256]{1,0:T(8,128)S(1)}, f32[]{:T(128)}) all-reduce(f32[32,256]{1,0:T(8,128)S(1)} %broadcast_multiply_fusion, f32[]{:T(128)} %get-tuple-element.130), channel_id=1, replica_groups=mesh['member'=4,'lat'=4,'lon'=2] {'member','lat','lon'}, use_global_device_ids=true, to_apply=%region_9.10 | all-reduce | flops 8193 | bytes 65544 | tf_op jit(solution)/shard_map/psum | solution.py:148
  138.6 98.4 %all-reduce.4.cloned.1.call-done = (f32[9,100,256]{2,1,0:T(8,128)}, f32[9,256,256]{2,1,0:T(8,128)}, f32[100,256]{1,0:T(8,128)}) async-done(((f32[9,100,256]{2,1,0:T(8,128)}, f32[9,256,256]{2,1,0:T(8,128)}, f32[100,256]{1,0:T(8,128)}), (f32[9,100,256]{2,1,0:T(8,128)}, f32[9,256,256]{2,1,0:T(8,128)}, f32[100,256]{1,0:T(8,128)})) %all-reduce.4.cloned.1.call-update) | async-done | bytes 3383312 | tf_op jit(solution)/shard_map/psum | solution.py:148
  237.0 2.2 multiply_reduce_fusion.1
  239.9 2.2 broadcast_divide_fusion.1
  244.0 1.6 broadcast_divide_fusion
  (189 shorter events, 38.2 us)
Async XLA Ops:
  7.2 43.9 %copy-start = (bf16[100,256]{1,0:T(8,128)(2,1)S(1)}, bf16[100,256]{1,0:T(8,128)(2,1)}, u32[]{:S(2)}) copy-start(bf16[100,256]{1,0:T(8,128)(2,1)} %param.16) | copy-start | bytes 153604
  7.2 229.8 %all-reduce.4.cloned.1.call-start = ((), (), s32[]{:S(2)}) async-start(), calls=%async_computation | async-start | bytes 6848512 | tf_op jit(solution)/shard_map/psum | solution.py:148
  8.5 6.8 %collective-permute-start.1 = (bf16[100,1,360]{2,1,0:T(2,128)(2,1)S(1)}, bf16[100,1,360]{2,1,0:T(2,128)(2,1)S(1)}, u32[]{:S(2)}, u32[]{:S(2)}) collective-permute-start(bf16[100,1,360]{2,1,0:T(2,128)(2,1)S(1)} %get-tuple-element.148), channel_id=1, source_target_pairs={{2,0},{4,2},{6,4},{0,6},{3,1},{5,3},{7,5},{1,7},{10,8},{12,10},{14... | collective-permute-start | bytes 216008 | tf_op jit(solution)/shard_map/ppermute | solution.py:18
  11.0 5.4 %collective-permute-start = (bf16[100,1,360]{2,1,0:T(2,128)(2,1)S(1)}, bf16[100,1,360]{2,1,0:T(2,128)(2,1)S(1)}, u32[]{:S(2)}, u32[]{:S(2)}) collective-permute-start(bf16[100,1,360]{2,1,0:T(2,128)(2,1)S(1)} %get-tuple-element.147), channel_id=1, source_target_pairs={{0,2},{2,4},{4,6},{6,0},{1,3},{3,5},{5,7},{7,1},{8,10},{10,12},{12... | collective-permute-start | bytes 216008 | tf_op jit(solution)/shard_map/ppermute | solution.py:15
  17.7 5.3 %collective-permute-start.3 = (bf16[100,4,1]{2,1,0:T(4,128)(2,1)S(1)}, bf16[100,4,1]{2,1,0:T(4,128)(2,1)S(1)}, u32[]{:S(2)}, u32[]{:S(2)}) collective-permute-start(bf16[100,4,1]{2,1,0:T(4,128)(2,1)S(1)} %get-tuple-element.133), channel_id=1, source_target_pairs={{1,0},{0,1},{3,2},{2,3},{5,4},{4,5},{7,6},{6,7},{9,8},{8,9},{11,10... | collective-permute-start | bytes 2408 | tf_op jit(solution)/shard_map/ppermute | solution.py:18
  19.2 4.8 %collective-permute-start.2 = (bf16[100,4,1]{2,1,0:T(4,128)(2,1)S(1)}, bf16[100,4,1]{2,1,0:T(4,128)(2,1)S(1)}, u32[]{:S(2)}, u32[]{:S(2)}) collective-permute-start(bf16[100,4,1]{2,1,0:T(4,128)(2,1)S(1)} %get-tuple-element.132), channel_id=1, source_target_pairs={{0,1},{1,0},{2,3},{3,2},{4,5},{5,4},{6,7},{7,6},{8,9},{9,8},{10,11... | collective-permute-start | bytes 2408 | tf_op jit(solution)/shard_map/ppermute | solution.py:15
  28.9 2.2 copy-start.21
  29.1 2.3 copy-start.19
  29.2 2.4 copy-start.37
  31.7 11.2 %copy-start.42 = (s32[2,360]{1,0:T(2,128)S(1)}, s32[2,360]{1,0:T(2,128)}, u32[]{:S(2)}) copy-start(s32[2,360]{1,0:T(2,128)} %param.12) | copy-start | bytes 8644
  31.7 11.2 %copy-start.2 = (bf16[100,2,360]{2,1,0:T(2,128)(2,1)S(1)}, bf16[100,2,360]{2,1,0:T(2,128)(2,1)}, u32[]{:S(2)}) copy-start(bf16[100,2,360]{2,1,0:T(2,128)(2,1)} %param.10) | copy-start | bytes 432004
  33.0 10.7 %copy-start.41 = (bf16[100,2,360]{2,1,0:T(2,128)(2,1)S(1)}, bf16[100,2,360]{2,1,0:T(2,128)(2,1)}, u32[]{:S(2)}) copy-start(bf16[100,2,360]{2,1,0:T(2,128)(2,1)} %param.11) | copy-start | bytes 432004
  33.0 5.4 %collective-permute-start.5 = (bf16[256,1,360]{0,2,1:T(8,128)(2,1)S(1)}, bf16[256,1,360]{0,2,1:T(8,128)(2,1)S(1)}, u32[]{:S(2)}, u32[]{:S(2)}) collective-permute-start(bf16[256,1,360]{0,2,1:T(8,128)(2,1)S(1)} %get-tuple-element.137), channel_id=1, source_target_pairs={{2,0},{4,2},{6,4},{0,6},{3,1},{5,3},{7,5},{1,7},{10,8},{12,10},{14... | collective-permute-start | bytes 552968 | tf_op jit(solution)/shard_map/ppermute | solution.py:18
  34.1 6.7 %collective-permute-start.4 = (bf16[256,1,360]{0,2,1:T(8,128)(2,1)S(1)}, bf16[256,1,360]{0,2,1:T(8,128)(2,1)S(1)}, u32[]{:S(2)}, u32[]{:S(2)}) collective-permute-start(bf16[256,1,360]{0,2,1:T(8,128)(2,1)S(1)} %get-tuple-element.136), channel_id=1, source_target_pairs={{0,2},{2,4},{4,6},{6,0},{1,3},{3,5},{5,7},{7,1},{8,10},{10,12},{12... | collective-permute-start | bytes 552968 | tf_op jit(solution)/shard_map/ppermute | solution.py:15
  40.8 3.9 %collective-permute-start.7 = (bf16[256,4,1]{0,2,1:T(2,128)(2,1)S(1)}, bf16[256,4,1]{0,2,1:T(2,128)(2,1)S(1)}, u32[]{:S(2)}, u32[]{:S(2)}) collective-permute-start(bf16[256,4,1]{0,2,1:T(2,128)(2,1)S(1)} %get-tuple-element.129), channel_id=1, source_target_pairs={{1,0},{0,1},{3,2},{2,3},{5,4},{4,5},{7,6},{6,7},{9,8},{8,9},{11,10... | collective-permute-start | bytes 6152 | tf_op jit(solution)/shard_map/ppermute | solution.py:18
  42.3 3.6 %collective-permute-start.6 = (bf16[256,4,1]{0,2,1:T(2,128)(2,1)S(1)}, bf16[256,4,1]{0,2,1:T(2,128)(2,1)S(1)}, u32[]{:S(2)}, u32[]{:S(2)}) collective-permute-start(bf16[256,4,1]{0,2,1:T(2,128)(2,1)S(1)} %get-tuple-element.128), channel_id=1, source_target_pairs={{0,1},{1,0},{2,3},{3,2},{4,5},{5,4},{6,7},{7,6},{8,9},{9,8},{10,11... | collective-permute-start | bytes 6152 | tf_op jit(solution)/shard_map/ppermute | solution.py:15
  46.8 2.2 copy-start.4
  46.8 3.0 %copy-start.17 = (bf16[256,2,360]{0,2,1:T(8,128)(2,1)}, bf16[256,2,360]{0,2,1:T(8,128)(2,1)S(1)}, u32[]{:S(2)}) copy-start(bf16[256,2,360]{0,2,1:T(8,128)(2,1)S(1)} %get-tuple-element.117) | copy-start | bytes 1105924
  76.9 4.4 %collective-permute-start.9 = (bf16[256,1,360]{0,2,1:T(8,128)(2,1)S(1)}, bf16[256,1,360]{0,2,1:T(8,128)(2,1)S(1)}, u32[]{:S(2)}, u32[]{:S(2)}) collective-permute-start(bf16[256,1,360]{0,2,1:T(8,128)(2,1)S(1)} %get-tuple-element.135), channel_id=1, source_target_pairs={{2,0},{4,2},{6,4},{0,6},{3,1},{5,3},{7,5},{1,7},{10,8},{12,10},{14... | collective-permute-start | bytes 552968 | tf_op jit(solution)/shard_map/ppermute | solution.py:18
  76.9 6.7 %collective-permute-start.8 = (bf16[256,1,360]{0,2,1:T(8,128)(2,1)S(1)}, bf16[256,1,360]{0,2,1:T(8,128)(2,1)S(1)}, u32[]{:S(2)}, u32[]{:S(2)}) collective-permute-start(bf16[256,1,360]{0,2,1:T(8,128)(2,1)S(1)} %get-tuple-element.134), channel_id=1, source_target_pairs={{0,2},{2,4},{4,6},{6,0},{1,3},{3,5},{5,7},{7,1},{8,10},{10,12},{12... | collective-permute-start | bytes 552968 | tf_op jit(solution)/shard_map/ppermute | solution.py:15
  80.1 7.2 %copy-start.14 = (f32[9,256,256]{2,1,0:T(8,128)}, f32[9,256,256]{2,1,0:T(8,128)S(1)}, u32[]{:S(2)}) copy-start(f32[9,256,256]{2,1,0:T(8,128)S(1)} %fusion.9) | copy-start | bytes 7077892
  83.7 3.7 %collective-permute-start.11 = (bf16[256,4,1]{0,2,1:T(2,128)(2,1)S(1)}, bf16[256,4,1]{0,2,1:T(2,128)(2,1)S(1)}, u32[]{:S(2)}, u32[]{:S(2)}) collective-permute-start(bf16[256,4,1]{0,2,1:T(2,128)(2,1)S(1)} %get-tuple-element.127), channel_id=1, source_target_pairs={{1,0},{0,1},{3,2},{2,3},{5,4},{4,5},{7,6},{6,7},{9,8},{8,9},{11,10... | collective-permute-start | bytes 6152 | tf_op jit(solution)/shard_map/ppermute | solution.py:18
  83.8 3.7 %collective-permute-start.10 = (bf16[256,4,1]{0,2,1:T(2,128)(2,1)S(1)}, bf16[256,4,1]{0,2,1:T(2,128)(2,1)S(1)}, u32[]{:S(2)}, u32[]{:S(2)}) collective-permute-start(bf16[256,4,1]{0,2,1:T(2,128)(2,1)S(1)} %get-tuple-element.126), channel_id=1, source_target_pairs={{0,1},{1,0},{2,3},{3,2},{4,5},{5,4},{6,7},{7,6},{8,9},{9,8},{10,11... | collective-permute-start | bytes 6152 | tf_op jit(solution)/shard_map/ppermute | solution.py:15
  237.0 5.1 %copy-start.1 = (f32[9,256,256]{2,1,0:T(8,128)S(1)}, f32[9,256,256]{2,1,0:T(8,128)}, u32[]{:S(2)}) copy-start(f32[9,256,256]{2,1,0:T(8,128)} %get-tuple-element.104) | copy-start | bytes 7077892
  (34 other events, 46.4 us)
Sparse Core Ops, SparseCore 0:
  95.2 141.7 all-reduce.3
where the time goes:
time: 256 us
  waiting for transfers between devices  119 us (46%)
  blocking collectives  57.6 us (22%)
  other arithmetic  20.7 us (8%)
  between operations  19.6 us (8%)
  matrix products  18.4 us (7%)
  starting transfers between devices  10.4 us (4%)
  local copies, waits for them, and re-layouts  9.45 us (4%)
    psum x1, waiting for transfers between devices, body(): lax.psum((grad_in, grad_mid, grad_out, grad_noise, loss_term), ('member',...  98.4 us
    psum x1, blocking collectives, body(): lax.psum((grad_in, grad_mid, grad_out, grad_noise, loss_term), ('member',...  40.8 us
    all_gather x1, blocking collectives, body(): lax.all_gather(output[None], 'member', axis=0, tiled=True)  16.8 us
    ppermute x6, waiting for transfers between devices, with_halo(): lax.ppermute(lax.slice_in_dim(block, 0, width, axis=dim), axis, backward)  12.8 us
    ppermute x6, waiting for transfers between devices, with_halo(): lax.ppermute(lax.slice_in_dim(block, block.shape[dim] - width, None, axis...  8.29 us
    dot_general x18, matrix products, conv_forward(): lax.dot_general(weights[offset], window, (((0,), (0,)), ((), ())), prefer...  6.96 us
    ppermute x6, starting transfers between devices, with_halo(): lax.ppermute(lax.slice_in_dim(block, 0, width, axis=dim), axis, backward)  6.79 us
  transfers between devices with their start and end apart: 13, of which 12 were waited for; matrix products, arithmetic and copies ran while one was open for 3% of the time, Pallas kernels for 0%

commit v1 on v0

--- a/solution.py
+++ b/solution.py
@@ -2,6 +2,7 @@
 import jax.numpy as jnp
 from jax import lax
 from jax.sharding import PartitionSpec as P
+from jax.lax import psum
 
 SMOOTH = 0.25
 
@@ -145,8 +146,9 @@
     grad_mid = weight_grad(hidden_pad, delta_mid, row_count, col_count)
     grad_in = weight_grad(state_pad, delta_in, row_count, col_count)
     grad_noise = latent[:, None] * jnp.sum(delta_in.astype(jnp.float32), axis=1)[None, :]
-    grad_in, grad_mid, grad_out, grad_noise, summed = lax.psum(
-        (grad_in, grad_mid, grad_out, grad_noise, loss_term), ("member", "lat", "lon")
+    grad_in, grad_mid, grad_out, grad_noise, summed = psum(
+        psum((grad_in, grad_mid, grad_out, grad_noise, loss_term), axis_name=("lat", "lon")),
+        axis_name="member",
     )
     loss = summed / (variables * cell_count * lat_count * lax.axis_size("lon"))
     return (

time: 256 us -> 324 us (1.27)
  waiting for transfers between devices: 119 us -> 177 us
  blocking collectives: 57.6 us -> 66 us
    psum x1 -> x2, waiting for transfers between devices: 98.4 us -> 156 us  [the longest x1 81.9 us: body(): psum(psum((grad_in, grad_mid, grad_out, grad_noise, loss_term), axis_name...]
    psum x1 -> x2, blocking collectives: 40.8 us -> 49.2 us  [the longest x1 26.7 us: body(): psum((grad_in, grad_mid, grad_out, grad_noise, loss_term), axis_name=('la...]
  transfers between devices with their start and end apart: 13 -> 14, of which waited for: 12 -> 13; matrix products, arithmetic and copies ran while one was open for 3% -> 2% of each run, Pallas kernels for 0% -> 0%
where the time goes in v1:
time: 324 us; the launch traced here: 323 us
  waiting for transfers between devices  177 us (55%)
  blocking collectives  66 us (20%)
  other arithmetic  20.7 us (6%)
  between operations  19.5 us (6%)
  matrix products  18.5 us (6%)
  local copies, waits for them, and re-layouts  10.9 us (3%)
  starting transfers between devices  10.4 us (3%)
    psum x1, waiting for transfers between devices, body(): psum(psum((grad_in, grad_mid, grad_out, grad_noise, loss_term), axis_name...  81.9 us
    psum x1, waiting for transfers between devices, body(): psum((grad_in, grad_mid, grad_out, grad_noise, loss_term), axis_name=('la...  74.2 us
    psum x1, blocking collectives, body(): psum((grad_in, grad_mid, grad_out, grad_noise, loss_term), axis_name=('la...  26.7 us
    psum x1, blocking collectives, body(): psum(psum((grad_in, grad_mid, grad_out, grad_noise, loss_term), axis_name...  22.6 us
    all_gather x1, blocking collectives, body(): lax.all_gather(output[None], 'member', axis=0, tiled=True)  16.7 us
    ppermute x6, waiting for transfers between devices, with_halo(): lax.ppermute(lax.slice_in_dim(block, 0, width, axis=dim), axis, backward)  12.7 us
    ppermute x6, waiting for transfers between devices, with_halo(): lax.ppermute(lax.slice_in_dim(block, block.shape[dim] - width, None, axis...  8.31 us
    dot_general x18, matrix products, conv_forward(): lax.dot_general(weights[offset], window, (((0,), (0,)), ((), ())), prefer...  6.98 us
  transfers between devices with their start and end apart: 14, of which 13 were waited for; matrix products, arithmetic and copies ran while one was open for 2% of the time, Pallas kernels for 0%

profile of v1, /device:TPU:0, one launch (start us, length us, event | category | flops | bytes accessed | tf_op | source)
XLA Modules:
  0.0 323.2 jit_solution(2839098449156446132)
XLA Ops:
  8.5 2.5 collective-permute-start.1
  11.9 3.4 %collective-permute-done.1 = bf16[100,1,360]{2,1,0:T(2,128)(2,1)S(1)} collective-permute-done((bf16[100,1,360]{2,1,0:T(2,128)(2,1)S(1)}, bf16[100,1,360]{2,1,0:T(2,128)(2,1)S(1)}, u32[]{:S(2)}, u32[]{:S(2)}) %collective-permute-start.1) | collective-permute-done | bytes 72032 | tf_op jit(solution)/shard_map/ppermute | solution.py:19
  17.7 1.6 collective-permute-start.3
  19.8 3.2 collective-permute-done.3
  24.1 2.2 maximum_select_fusion.2
  26.3 1.4 fusion.123
  31.7 1.3 multiply_convert_fusion
  34.1 4.3 %collective-permute-done.5 = bf16[256,1,360]{0,2,1:T(8,128)(2,1)S(1)} collective-permute-done((bf16[256,1,360]{0,2,1:T(8,128)(2,1)S(1)}, bf16[256,1,360]{0,2,1:T(8,128)(2,1)S(1)}, u32[]{:S(2)}, u32[]{:S(2)}) %collective-permute-start.5) | collective-permute-done | bytes 184352 | tf_op jit(solution)/shard_map/ppermute | solution.py:19
  38.4 2.3 collective-permute-done.4
  40.8 1.6 collective-permute-start.7
  49.8 1.3 add_convert_fusion
  52.2 16.7 %all-gather.1 = bf16[4,100,720]{2,1,0:T(8,128)(2,1)} all-gather(bf16[1,100,720]{2,1,0:T(8,128)(2,1)S(1)} %bitcast.306), channel_id=2, replica_groups=mesh['member'=4,'lat'=4,'lon'=2] {'member'}, dimensions={0}, use_global_device_ids=true | all-gather | bytes 720000 | tf_op jit(solution)/shard_map/all_gather | solution.py:129
  68.9 4.7 %while.15 = (s32[]{:T(128)}, f32[1,100,720]{2,1,0:T(8,128)S(1)}, f32[1,100,720]{2,1,0:T(8,128)S(1)}, bf16[4,100,720]{2,1,0:T(8,128)(2,1)}, f32[1,100,720]{2,1,0:T(8,128)S(1)}, /*index=5*/s32[]{:T(128)}, s32[]{:T(128)}) while((s32[]{:T(128)}, f32[1,100,720]{2,1,0:T(8,128)S(1)}, f32[1,100,720]{2,1,0:T(8,128)S(1)}, ...), condition=%wide.region_1.2_spmd.clone, body=%wide.region_0.1_spmd.clone.sunk | while | flops 720003 | bytes 1584099 | solution.py:91
  73.7 1.8 fusion.51
  75.5 1.7 fusion.49
  82.0 2.5 collective-permute-done.8
  84.6 1.9 collective-permute-start.10
  95.9 74.2 %all-reduce.7.cloned.1.call-done = (f32[9,100,256]{2,1,0:T(8,128)}, f32[9,256,256]{2,1,0:T(8,128)}, f32[100,256]{1,0:T(8,128)}) async-done(((f32[9,100,256]{2,1,0:T(8,128)}, f32[9,256,256]{2,1,0:T(8,128)}, f32[100,256]{1,0:T(8,128)}), (f32[9,100,256]{2,1,0:T(8,128)}, f32[9,256,256]{2,1,0:T(8,128)}, f32[100,256]{1,0:T(8,128)})) %all-reduce.7.cloned.1.call-update) | async-done | bytes 3383312 | tf_op jit(solution)/shard_map/psum | solution.py:150
  170.9 26.7 %all-reduce = (f32[32,256]{1,0:T(8,128)S(1)}, f32[]{:T(128)}) all-reduce(f32[32,256]{1,0:T(8,128)S(1)} %broadcast_multiply_fusion, f32[]{:T(128)} %get-tuple-element.135), channel_id=1, replica_groups=mesh['member'=4,'lat'=4,'lon'=2] {'lat','lon'}, use_global_device_ids=true, to_apply=%region_12.13 | all-reduce | flops 8193 | bytes 65544 | tf_op jit(solution)/shard_map/psum | solution.py:150
  197.5 22.6 %all-reduce.2 = (f32[32,256]{1,0:T(8,128)S(1)}, f32[]{:T(128)}) all-reduce(f32[32,256]{1,0:T(8,128)S(1)} %get-tuple-element.101, f32[]{:T(128)} %get-tuple-element.102), channel_id=1, replica_groups=mesh['member'=4,'lat'=4,'lon'=2] {'member'}, use_global_device_ids=true, to_apply=%region_13.14 | all-reduce | flops 8193 | bytes 65544 | tf_op jit(solution)/shard_map/psum | solution.py:149
  222.7 81.9 %all-reduce.9.cloned.1.call-done = (f32[9,100,256]{2,1,0:T(8,128)}, f32[9,256,256]{2,1,0:T(8,128)}, f32[100,256]{1,0:T(8,128)}) async-done(((f32[9,100,256]{2,1,0:T(8,128)}, f32[9,256,256]{2,1,0:T(8,128)}, f32[100,256]{1,0:T(8,128)}), (f32[9,100,256]{2,1,0:T(8,128)}, f32[9,256,256]{2,1,0:T(8,128)}, f32[100,256]{1,0:T(8,128)})) %all-reduce.9.cloned.1.call-update) | async-done | bytes 3383312 | tf_op jit(solution)/shard_map/psum | solution.py:149
  304.6 2.2 multiply_reduce_fusion.1
  307.5 2.2 broadcast_divide_fusion.1
  311.6 1.6 broadcast_divide_fusion
  (193 shorter events, 42.4 us)
Async XLA Ops:
  7.2 44.7 %copy-start = (bf16[100,256]{1,0:T(8,128)(2,1)S(1)}, bf16[100,256]{1,0:T(8,128)(2,1)}, u32[]{:S(2)}) copy-start(bf16[100,256]{1,0:T(8,128)(2,1)} %param.16) | copy-start | bytes 153604
  7.2 163.0 %all-reduce.7.cloned.1.call-start = ((), (), s32[]{:S(2)}) async-start(), calls=%async_computation | async-start | bytes 6848512 | tf_op jit(solution)/shard_map/psum | solution.py:150
  8.5 6.8 %collective-permute-start.1 = (bf16[100,1,360]{2,1,0:T(2,128)(2,1)S(1)}, bf16[100,1,360]{2,1,0:T(2,128)(2,1)S(1)}, u32[]{:S(2)}, u32[]{:S(2)}) collective-permute-start(bf16[100,1,360]{2,1,0:T(2,128)(2,1)S(1)} %get-tuple-element.153), channel_id=1, source_target_pairs={{2,0},{4,2},{6,4},{0,6},{3,1},{5,3},{7,5},{1,7},{10,8},{12,10},{14... | collective-permute-start | bytes 216008 | tf_op jit(solution)/shard_map/ppermute | solution.py:19
  11.0 5.4 %collective-permute-start = (bf16[100,1,360]{2,1,0:T(2,128)(2,1)S(1)}, bf16[100,1,360]{2,1,0:T(2,128)(2,1)S(1)}, u32[]{:S(2)}, u32[]{:S(2)}) collective-permute-start(bf16[100,1,360]{2,1,0:T(2,128)(2,1)S(1)} %get-tuple-element.152), channel_id=1, source_target_pairs={{0,2},{2,4},{4,6},{6,0},{1,3},{3,5},{5,7},{7,1},{8,10},{10,12},{12... | collective-permute-start | bytes 216008 | tf_op jit(solution)/shard_map/ppermute | solution.py:16
  17.7 5.3 %collective-permute-start.3 = (bf16[100,4,1]{2,1,0:T(4,128)(2,1)S(1)}, bf16[100,4,1]{2,1,0:T(4,128)(2,1)S(1)}, u32[]{:S(2)}, u32[]{:S(2)}) collective-permute-start(bf16[100,4,1]{2,1,0:T(4,128)(2,1)S(1)} %get-tuple-element.138), channel_id=1, source_target_pairs={{1,0},{0,1},{3,2},{2,3},{5,4},{4,5},{7,6},{6,7},{9,8},{8,9},{11,10... | collective-permute-start | bytes 2408 | tf_op jit(solution)/shard_map/ppermute | solution.py:19
  19.2 4.8 %collective-permute-start.2 = (bf16[100,4,1]{2,1,0:T(4,128)(2,1)S(1)}, bf16[100,4,1]{2,1,0:T(4,128)(2,1)S(1)}, u32[]{:S(2)}, u32[]{:S(2)}) collective-permute-start(bf16[100,4,1]{2,1,0:T(4,128)(2,1)S(1)} %get-tuple-element.137), channel_id=1, source_target_pairs={{0,1},{1,0},{2,3},{3,2},{4,5},{5,4},{6,7},{7,6},{8,9},{9,8},{10,11... | collective-permute-start | bytes 2408 | tf_op jit(solution)/shard_map/ppermute | solution.py:16
  29.2 2.4 copy-start.37
  31.7 11.2 %copy-start.42 = (s32[2,360]{1,0:T(2,128)S(1)}, s32[2,360]{1,0:T(2,128)}, u32[]{:S(2)}) copy-start(s32[2,360]{1,0:T(2,128)} %param.12) | copy-start | bytes 8644
  31.7 11.2 %copy-start.2 = (bf16[100,2,360]{2,1,0:T(2,128)(2,1)S(1)}, bf16[100,2,360]{2,1,0:T(2,128)(2,1)}, u32[]{:S(2)}) copy-start(bf16[100,2,360]{2,1,0:T(2,128)(2,1)} %param.10) | copy-start | bytes 432004
  33.0 10.7 %copy-start.41 = (bf16[100,2,360]{2,1,0:T(2,128)(2,1)S(1)}, bf16[100,2,360]{2,1,0:T(2,128)(2,1)}, u32[]{:S(2)}) copy-start(bf16[100,2,360]{2,1,0:T(2,128)(2,1)} %param.11) | copy-start | bytes 432004
  33.0 5.4 %collective-permute-start.5 = (bf16[256,1,360]{0,2,1:T(8,128)(2,1)S(1)}, bf16[256,1,360]{0,2,1:T(8,128)(2,1)S(1)}, u32[]{:S(2)}, u32[]{:S(2)}) collective-permute-start(bf16[256,1,360]{0,2,1:T(8,128)(2,1)S(1)} %get-tuple-element.142), channel_id=1, source_target_pairs={{2,0},{4,2},{6,4},{0,6},{3,1},{5,3},{7,5},{1,7},{10,8},{12,10},{14... | collective-permute-start | bytes 552968 | tf_op jit(solution)/shard_map/ppermute | solution.py:19
  34.1 6.7 %collective-permute-start.4 = (bf16[256,1,360]{0,2,1:T(8,128)(2,1)S(1)}, bf16[256,1,360]{0,2,1:T(8,128)(2,1)S(1)}, u32[]{:S(2)}, u32[]{:S(2)}) collective-permute-start(bf16[256,1,360]{0,2,1:T(8,128)(2,1)S(1)} %get-tuple-element.141), channel_id=1, source_target_pairs={{0,2},{2,4},{4,6},{6,0},{1,3},{3,5},{5,7},{7,1},{8,10},{10,12},{12... | collective-permute-start | bytes 552968 | tf_op jit(solution)/shard_map/ppermute | solution.py:16
  40.8 3.9 %collective-permute-start.7 = (bf16[256,4,1]{0,2,1:T(2,128)(2,1)S(1)}, bf16[256,4,1]{0,2,1:T(2,128)(2,1)S(1)}, u32[]{:S(2)}, u32[]{:S(2)}) collective-permute-start(bf16[256,4,1]{0,2,1:T(2,128)(2,1)S(1)} %get-tuple-element.134), channel_id=1, source_target_pairs={{1,0},{0,1},{3,2},{2,3},{5,4},{4,5},{7,6},{6,7},{9,8},{8,9},{11,10... | collective-permute-start | bytes 6152 | tf_op jit(solution)/shard_map/ppermute | solution.py:19
  42.3 3.6 %collective-permute-start.6 = (bf16[256,4,1]{0,2,1:T(2,128)(2,1)S(1)}, bf16[256,4,1]{0,2,1:T(2,128)(2,1)S(1)}, u32[]{:S(2)}, u32[]{:S(2)}) collective-permute-start(bf16[256,4,1]{0,2,1:T(2,128)(2,1)S(1)} %get-tuple-element.133), channel_id=1, source_target_pairs={{0,1},{1,0},{2,3},{3,2},{4,5},{5,4},{6,7},{7,6},{8,9},{9,8},{10,11... | collective-permute-start | bytes 6152 | tf_op jit(solution)/shard_map/ppermute | solution.py:16
  46.8 2.2 copy-start.4
  46.8 3.0 copy-start.19
  77.6 4.3 %collective-permute-start.9 = (bf16[256,1,360]{0,2,1:T(8,128)(2,1)S(1)}, bf16[256,1,360]{0,2,1:T(8,128)(2,1)S(1)}, u32[]{:S(2)}, u32[]{:S(2)}) collective-permute-start(bf16[256,1,360]{0,2,1:T(8,128)(2,1)S(1)} %get-tuple-element.140), channel_id=1, source_target_pairs={{2,0},{4,2},{6,4},{0,6},{3,1},{5,3},{7,5},{1,7},{10,8},{12,10},{14... | collective-permute-start | bytes 552968 | tf_op jit(solution)/shard_map/ppermute | solution.py:19
  77.7 6.7 %collective-permute-start.8 = (bf16[256,1,360]{0,2,1:T(8,128)(2,1)S(1)}, bf16[256,1,360]{0,2,1:T(8,128)(2,1)S(1)}, u32[]{:S(2)}, u32[]{:S(2)}) collective-permute-start(bf16[256,1,360]{0,2,1:T(8,128)(2,1)S(1)} %get-tuple-element.139), channel_id=1, source_target_pairs={{0,2},{2,4},{4,6},{6,0},{1,3},{3,5},{5,7},{7,1},{8,10},{10,12},{12... | collective-permute-start | bytes 552968 | tf_op jit(solution)/shard_map/ppermute | solution.py:16
  80.2 6.3 %copy-start.16 = (bf16[256,720]{0,1:T(8,128)(2,1)S(1)}, bf16[256,720]{0,1:T(8,128)(2,1)}, u32[]{:S(2)}) copy-start(bf16[256,720]{0,1:T(8,128)(2,1)} %copy-done.15) | copy-start | bytes 1105924
  80.9 7.2 %copy-start.14 = (f32[9,256,256]{2,1,0:T(8,128)}, f32[9,256,256]{2,1,0:T(8,128)S(1)}, u32[]{:S(2)}) copy-start(f32[9,256,256]{2,1,0:T(8,128)S(1)} %fusion.9) | copy-start | bytes 7077892
  84.4 3.7 %collective-permute-start.11 = (bf16[256,4,1]{0,2,1:T(2,128)(2,1)S(1)}, bf16[256,4,1]{0,2,1:T(2,128)(2,1)S(1)}, u32[]{:S(2)}, u32[]{:S(2)}) collective-permute-start(bf16[256,4,1]{0,2,1:T(2,128)(2,1)S(1)} %get-tuple-element.132), channel_id=1, source_target_pairs={{1,0},{0,1},{3,2},{2,3},{5,4},{4,5},{7,6},{6,7},{9,8},{8,9},{11,10... | collective-permute-start | bytes 6152 | tf_op jit(solution)/shard_map/ppermute | solution.py:19
  84.6 3.6 %collective-permute-start.10 = (bf16[256,4,1]{0,2,1:T(2,128)(2,1)S(1)}, bf16[256,4,1]{0,2,1:T(2,128)(2,1)S(1)}, u32[]{:S(2)}, u32[]{:S(2)}) collective-permute-start(bf16[256,4,1]{0,2,1:T(2,128)(2,1)S(1)} %get-tuple-element.131), channel_id=1, source_target_pairs={{0,1},{1,0},{2,3},{3,2},{4,5},{5,4},{6,7},{7,6},{8,9},{9,8},{10,11... | collective-permute-start | bytes 6152 | tf_op jit(solution)/shard_map/ppermute | solution.py:16
  95.9 208.7 %all-reduce.9.cloned.1.call-start = ((), (), s32[]{:S(2)}) async-start(), calls=%async_computation.1 | async-start | bytes 6848512 | tf_op jit(solution)/shard_map/psum | solution.py:149
  304.6 5.1 %copy-start.1 = (f32[9,256,256]{2,1,0:T(8,128)S(1)}, f32[9,256,256]{2,1,0:T(8,128)}, u32[]{:S(2)}) copy-start(f32[9,256,256]{2,1,0:T(8,128)} %get-tuple-element.109) | copy-start | bytes 7077892
  (35 other events, 48.6 us)
Sparse Core Ops, SparseCore 0:
  96.0 74.0 all-reduce.6
  172.7 131.8 all-reduce.8
